TPU v7x, 32 devices: a whole 2x2x4 slice. The times are simulated.
32 devices in a mesh: orb: 16 (over z, y, core), grid: 2 (over x).
Axes of the slice: x: 2, y: 2, z: 4, core: 2. Of those that a mesh axis runs over, the one named last changes fastest.
Arguments:
- orbitals: bfloat16 [32, 11520], P('orb', 'grid'), may hold values from -1.5 to 1.5
- occupation: bfloat16 [32], P('orb'), may hold values from 0.29882812 to 1
Outputs:
- potentials: float32 [32, 11520], P('orb', 'grid')
- projectors: float32 [32, 11520], P('orb', 'grid')
All inputs are finite; a program needn't handle non-finite values.
Results may differ from a plain program's by a relative error of at most 0.0025.
Values may be sent and summed in bfloat16 or wider, within the bound.
A program may use at most 64 MiB of HBM per device.

v0:
```python
import functools
import math

import jax
import jax.numpy as jnp
import numpy as np
from jax import lax
from jax.experimental import pallas as pl
from jax.experimental.pallas import tpu as pltpu
from jax.sharding import PartitionSpec as P

NX = 20
NY = 24
NZ = 24
NPTS = NX * NY * NZ
PLANE = NY * NZ
HALVES = 2
HX = NX // HALVES
TILE = 8
EDGE = HX - TILE
ROWS = 3 * TILE
LANES = 128
BATCH = 8
MESH = pl.DeviceIdType.MESH


def hartley_table(length):
    index = np.arange(length, dtype=np.int32)
    product = index[:, None] * index[None, :] % length
    angle = np.float32(2.0 * math.pi / length) * product.astype(np.float32)
    return np.cos(angle) + np.sin(angle)


def signed_square(length):
    index = np.arange(length, dtype=np.int32)
    signed = np.where(index <= length // 2, index, index - length).astype(np.float32)
    return (np.float32(2.0 * math.pi) * signed / np.float32(length)) ** 2


def padded_rows(array):
    zero = np.zeros((TILE - 2 * EDGE,) + array.shape[1:], array.dtype)
    first, second = array[:HX], array[HX:]
    parts = [first[:TILE], first[TILE:], second[TILE:], zero, second[:TILE]]
    return np.concatenate(parts, axis=0)


def tables():
    table_x = padded_rows(padded_rows(hartley_table(NX)).T)
    table_x = np.kron(np.eye(BATCH, dtype=np.float32), table_x)
    table_y = np.kron(hartley_table(NY), np.eye(NZ, dtype=np.float32))
    table_z = np.kron(np.eye(16, dtype=np.float32), hartley_table(NZ))
    total = (
        signed_square(NX)[:, None, None]
        + signed_square(NY)[None, :, None]
        + signed_square(NZ)[None, None, :]
    )
    safe = np.where(total > 0, total, 1.0)
    kernel = np.where(total > 0, 1.0 / safe, 0.0) / NPTS
    kernel = padded_rows(kernel.reshape(NX, PLANE).astype(np.float32))
    return (
        jnp.asarray(table_x, jnp.bfloat16),
        jnp.asarray(table_y, jnp.bfloat16),
        jnp.asarray(table_z, jnp.bfloat16),
        jnp.asarray(kernel, jnp.float32),
    )


def column_of(matrix, k):
    if isinstance(k, int):
        return matrix[:, k : k + 1]
    lane = lax.broadcasted_iota(jnp.int32, matrix.shape, 1)
    return jnp.sum(jnp.where(lane == k, matrix, 0.0), axis=1, keepdims=True)


def row_of(matrix, k):
    if isinstance(k, int):
        return matrix[k : k + 1, :]
    line = lax.broadcasted_iota(jnp.int32, matrix.shape, 0)
    return jnp.sum(jnp.where(line == k, matrix, 0.0), axis=0, keepdims=True)


def loop(count, body, carry, most=64):
    if count <= most:
        for k in range(count):
            carry = body(k, carry)
        return carry
    return lax.fori_loop(0, count, body, carry)


def body(
    cols,
    own_ref,
    occ_ref,
    tx_hbm,
    ty_hbm,
    tz_hbm,
    k_hbm,
    pot_out,
    proj_out,
    pot_ref,
    proj_ref,
    s_o,
    tx_ref,
    ty_ref,
    tz_ref,
    k_ref,
    src,
    part,
    part_in,
    pots,
    pedge,
    edge_out,
    edge_in,
    rowsum,
    gown,
    gall,
    gmat,
    s_tab,
    s_x,
    r_x,
    s_a,
    s_y,
    s_c,
    r_col,
    r_y,
    r_core,
    s_p,
    r_p,
    s_g,
    r_g,
    t_a,
    t_y,
    t_c,
    t_col,
    t_yin,
    t_core,
):
    o = lax.axis_index("orb")
    g = lax.axis_index("grid")
    n_orb = 4 * cols
    n = 2 * n_orb
    r = o // 4
    y = (o % 4) // 2
    c = o % 2
    h = 1 - g
    f32 = jnp.float32
    bf16 = jnp.bfloat16
    o_y = r * 4 + (1 - y) * 2 + c
    o_c = r * 4 + y * 2 + (1 - c)

    loads = [
        pltpu.make_async_copy(a, b, s_tab.at[i])
        for i, (a, b) in enumerate(
            ((tx_hbm, tx_ref), (ty_hbm, ty_ref), (tz_hbm, tz_ref), (k_hbm, k_ref))
        )
    ]
    for load in loads:
        load.start()

    barrier = pltpu.get_barrier_semaphore()

    def greet(orb, grid):
        pl.semaphore_signal(barrier, inc=1, device_id=(orb, grid), device_id_type=MESH)

    @pl.loop(1, cols)
    def _(d):
        greet((r + d) % cols * 4 + y * 2 + c, g)

    greet(o, h)
    greet(o_y, g)
    greet(o_c, g)

    own = own_ref[...].astype(f32)
    occ = occ_ref[...].astype(f32)
    own_edges = []
    for t in range(2):
        lines = [own[t : t + 1, PLANE * x : PLANE * (x + 1)] for x in range(HX)]
        src[r, y, c, t, 2 * g] = jnp.concatenate(lines[:TILE], axis=0).astype(bf16)
        own_edges += lines[TILE:]
    own_edges = jnp.concatenate(own_edges + [jnp.zeros((2 * EDGE, PLANE), f32)], axis=0)
    edge_out[...] = own_edges.astype(bf16)

    pl.semaphore_wait(barrier, cols + 2)

    def copy(source, target, send, recv, orb, grid):
        return pltpu.make_async_remote_copy(
            src_ref=source,
            dst_ref=target,
            send_sem=send,
            recv_sem=recv,
            device_id=(orb, grid),
            device_id_type=MESH,
        )

    def piece(j, q, u, w):
        if j == 0:
            return src.at[q, u, w, g, 2 * g]
        if j == 1:
            return src.at[q, u, w, g, pl.ds(h, 2)]
        return src.at[q, u, w, h, pl.ds(g, 2)]

    def same(ref, send, recv, orb):
        return copy(ref, ref, send, recv, orb, g)

    def to_column(j, d):
        q = (r + d) % cols
        return same(piece(j, r, y, c), s_a.at[j], r_col.at[j, r], q * 4 + y * 2 + c)

    def to_y(j, q):
        return same(piece(j, q, y, c), s_y.at[j], r_y.at[j, q], o_y)

    def to_core(j, q, u):
        return same(piece(j, q, u, c), s_c.at[j], r_core.at[j, u], o_c)

    def arrived(j, q, u, w, recv):
        same(piece(j, q, u, w), s_a.at[j], recv, o_c).wait_recv()

    everyone = pl.ds(0, cols)
    others = pl.ds(0, cols - 1)
    both = pl.ds(0, 2)

    def crossing(half):
        tile = src.at[r, y, c, :, 2 * half]
        return copy(tile, tile, s_x.at[0], r_x.at[0], o, h)

    crosses = (crossing(g), copy(edge_out, edge_in, s_x.at[1], r_x.at[1], o, h))
    for cross in crosses:
        cross.start()

    def send_own(j):
        @pl.loop(1, cols)
        def _(d):
            to_column(j, cols - d).start()

        to_y(j, r).start()
        to_core(j, r, y).start()

    send_own(0)
    crossing(h).wait_recv()
    crosses[1].wait_recv()
    second_half = g.astype(f32)
    first_half = 1.0 - second_half
    edges = edge_in[...].astype(f32)
    low = own_edges * first_half + edges * second_half
    high = edges * first_half + own_edges * second_half
    for t in range(2):
        own_lines = slice(EDGE * t, EDGE * (t + 1))
        lines = [low[own_lines], high[own_lines]]
        lines.append(jnp.broadcast_to(occ[:, t : t + 1], (1, PLANE)))
        lines.append(jnp.zeros((TILE - 2 * EDGE - 1, PLANE), f32))
        src[r, y, c, t, 1] = jnp.concatenate(lines, axis=0).astype(bf16)
    send_own(1)

    def relay_column(j):
        @pl.loop(1, cols)
        def _(d):
            q = (r + d) % cols
            arrived(j, q, y, c, r_col.at[j, q])
            to_y(j, q).start()
            to_core(j, q, y).start()

    def relay_y(j):
        @pl.loop(0, cols)
        def _(d):
            q = (r + d) % cols
            arrived(j, q, 1 - y, c, r_y.at[j, q])
            to_core(j, q, 1 - y).start()

    def other_core(j, u):
        arrived(j, everyone, u, 1 - c, r_core.at[j, u])

    relay_column(0)
    relay_column(1)
    send_own(2)
    for load in loads:
        load.wait()
    other_core(0, y)
    other_core(1, y)

    tx = tx_ref[...]
    ty = ty_ref[...]
    tz = tz_ref[...]
    cut = tz.shape[0]
    rest = PLANE - cut
    kern = k_ref[...]

    def mm(a, b):
        return jnp.dot(a, b, preferred_element_type=f32)

    def along_z(a):
        return jnp.concatenate([mm(a[:, :cut], tz), mm(a[:, cut:], tz[:rest, :rest])], axis=1)

    per = BATCH // 2
    block = (BATCH, ROWS, PLANE)
    flat_block = (BATCH * ROWS, PLANE)
    steps = cols // per

    def one_batch(u, step, t, first):
        raw = src[pl.ds(step * per, per), u, :, g].reshape(BATCH * 3, TILE, PLANE)
        raw = raw.astype(f32).reshape(block)
        weight = raw[:, TILE + 2 * EDGE : TILE + 2 * EDGE + 1, :]
        target = src[r, y, c, t].astype(f32).reshape(block[1:])
        density = (raw * target[None]).reshape(flat_block).astype(bf16)
        s = mm(tx, density).astype(bf16)
        s = mm(s, ty).astype(bf16)
        s = along_z(s).reshape(block) * kern[None]
        s = along_z(s.reshape(flat_block).astype(bf16)).astype(bf16)
        s = mm(s, ty).astype(bf16)
        v = mm(tx, s).reshape(block)
        total = jnp.sum(weight * v * raw, axis=0).reshape(3, TILE, PLANE)
        if first:
            part[t] = -total
        else:
            part[t] -= total

    def batches(u, t, first):
        if first:
            one_batch(u, 0, t, True)
        if steps > int(first):

            @pl.loop(int(first), steps)
            def _(k):
                one_batch(u, k, t, False)

    batches(y, 0, True)
    relay_y(0)
    relay_y(1)
    batches(y, 1, True)
    relay_column(2)
    other_core(0, 1 - y)
    other_core(1, 1 - y)
    batches(1 - y, 0, False)

    def swap(t):
        return copy(part.at[t, pl.ds(h, 2)], part_in.at[t], s_p.at[t], r_p.at[t], o, h)

    swap(0).start()
    batches(1 - y, 1, False)
    swap(1).start()

    relay_y(2)

    def pot_at(t, q, u, w):
        return pedge.at[q, u, w] if t == 2 else pots.at[q, u, w, t]

    def pot_column(t, d):
        q = (r + d) % cols
        return same(pot_at(t, r, y, c), t_a.at[t], t_col.at[t, r], q * 4 + y * 2 + c)

    def pot_y(t, q):
        return same(pot_at(t, q, y, c), t_y.at[t], t_yin.at[t, q], o_y)

    def pot_core(t, q, u):
        return same(pot_at(t, q, u, c), t_c.at[t], t_core.at[t, u], o_c)

    def pot_arrived(t, q, u, w, recv):
        same(pot_at(t, q, u, w), t_a.at[t], recv, o_c).wait_recv()

    def send_pots(t):
        @pl.loop(1, cols)
        def _(d):
            pot_column(t, cols - d).start()

        pot_y(t, r).start()
        pot_core(t, r, y).start()

    def gram_rows(t, value):
        @pl.loop(0, cols)
        def _(q):
            rows = src[q, :, :, :, 2 * g].reshape(8, TILE, PLANE).astype(f32)
            ends = src[q, :, :, :, 1].reshape(8, TILE, PLANE).astype(f32)
            sums = jnp.sum(rows * value[0][None] + ends * value[2][None], axis=1)
            fold = sums[:, :LANES]
            for k in range(LANES, PLANE - LANES + 1, LANES):
                fold += sums[:, k : k + LANES]
            tail = PLANE % LANES
            if tail:
                last = jnp.zeros((8, LANES - tail), f32)
                fold += jnp.concatenate([sums[:, PLANE - tail :], last], axis=1)
            rowsum[t, pl.ds(pl.multiple_of(q * 8, 8), 8), :] = fold

        gown[t : t + 1, :] = jnp.sum(rowsum[t].T, axis=0, keepdims=True)

    def finish(t):
        swap(t).wait_recv()
        tile = part[t, 2 * g] + part_in[t, g]
        pots[r, y, c, t] = tile
        rest = part[t, 1] + part_in[t, h]
        edge = rest[:EDGE] * first_half + rest[EDGE : 2 * EDGE] * second_half
        line = lax.broadcasted_iota(jnp.int32, (TILE, PLANE), 0)
        return tile, edge, jnp.where(line // EDGE == g, rest, 0.0)

    value0 = finish(0)
    send_pots(0)
    other_core(2, y)
    other_core(2, 1 - y)
    gram_rows(0, value0)
    value1 = finish(1)
    send_pots(1)
    gram_rows(1, value1)
    gall[g * n_orb + o] = gown[...]

    def gram_to(d):
        flat = (o * 2 + g + d) % (2 * n_orb)
        return copy(gown, gall.at[g * n_orb + o], s_g, r_g, flat // 2, flat % 2)

    @pl.loop(1, 2 * n_orb)
    def _(d):
        gram_to(d).start()

    pedge[r, y, c] = jnp.concatenate([value0[1], value1[1]], axis=0)
    send_pots(2)

    def write(ref, t, value):
        for x in range(0, HX, 2):
            pair = jnp.concatenate([value[x : x + 1], value[x + 1 : x + 2]], axis=1)
            ref[t : t + 1, PLANE * x : PLANE * (x + 2)] = pair

    write(pot_ref, 0, jnp.concatenate(value0[:2], axis=0))
    write(pot_ref, 1, jnp.concatenate(value1[:2], axis=0))
    store_pot = pltpu.make_async_copy(pot_ref, pot_out, s_o.at[0])
    store_pot.start()

    def pot_relay_column(t):
        @pl.loop(1, cols)
        def _(d):
            q = (r + d) % cols
            pot_arrived(t, q, y, c, t_col.at[t, q])
            pot_y(t, q).start()
            pot_core(t, q, y).start()

    def pot_relay_y(t):
        @pl.loop(0, cols)
        def _(d):
            q = (r + d) % cols
            pot_arrived(t, q, 1 - y, c, t_yin.at[t, q])
            pot_core(t, q, 1 - y).start()

    pot_relay_column(0)
    pot_relay_column(1)
    pot_relay_column(2)
    pot_relay_y(0)

    for cross in crosses:
        cross.wait_send()
    for t in range(2):
        swap(t).wait_send()

    for j in range(3):
        same(piece(j, others, y, c), s_a.at[j], r_col.at[j, r], o_c).wait_send()
        same(piece(j, everyone, y, c), s_y.at[j], r_col.at[j, r], o_c).wait_send()
        same(piece(j, everyone, both, c), s_c.at[j], r_col.at[j, r], o_c).wait_send()

    received = gall.at[pl.ds(0, 2 * n_orb - 1)]
    grams = copy(received, received, s_g, r_g, o_c, g)
    grams.wait_recv()

    def assemble(k, carry):
        pairs = [gall[4 * k + j] + gall[n_orb + 4 * k + j] for j in range(4)]
        start = 8 * k if isinstance(k, int) else pl.multiple_of(8 * k, 8)
        gmat[pl.ds(start, 8), :] = jnp.concatenate(pairs, axis=0)
        return carry

    loop(cols, assemble, 0, 16)
    gram = gmat[...]
    sym = (gram + gram.T) * f32(-0.5 / NPTS)
    row_id = lax.broadcasted_iota(jnp.int32, (n, n), 0)
    eye = (row_id == lax.broadcasted_iota(jnp.int32, (n, n), 1)).astype(f32)
    below = lax.broadcasted_iota(jnp.int32, (n, 1), 0)

    def eliminate(k, pair):
        left, right = pair
        row_l = row_of(left, k)
        scale = 1.0 / column_of(row_l, k)
        factor = jnp.where(below > k, column_of(left, k) * scale, 0.0)
        return left - factor * row_l, right - factor * row_of(right, k)

    early = n * 3 // 4
    if n <= 64:
        pair = loop(early, eliminate, (sym, eye))
        pot_relay_y(1)
        pot_relay_y(2)
        for k in range(early, n):
            pair = eliminate(k, pair)
        left, right = pair
    else:
        pot_relay_y(1)
        pot_relay_y(2)
        left, right = loop(n, eliminate, (sym, eye))
    diag = jnp.sum(left * eye, axis=1, keepdims=True)
    inverse = right * (1.0 / jnp.sqrt(diag))
    a0, a1 = row_of(inverse, 2 * o), row_of(inverse, 2 * o + 1)

    for u in range(2):
        for t in range(3):
            pot_arrived(t, everyone, u, 1 - c, t_core.at[t, u])

    def add(k, sums):
        where = (k // 4, k % 4 // 2, k % 2)
        if not isinstance(k, int):
            where = (k // 4, lax.rem(k, 4) // 2, lax.rem(k, 2))
        edge = pedge[where]
        tiles = [pots[where + (t,)] for t in range(2)]
        ends = [edge[EDGE * t : EDGE * (t + 1)] for t in range(2)]
        new = []
        for a, (tile, end) in zip((a0, a1), sums):
            for t in range(2):
                factor = column_of(a, 2 * k + t)
                tile, end = tile + factor * tiles[t], end + factor * ends[t]
            new.append((tile, end))
        return tuple(new)

    zero = (jnp.zeros((TILE, PLANE), f32), jnp.zeros((EDGE, PLANE), f32))
    proj = loop(n_orb, add, (zero, zero))
    for t in range(2):
        write(proj_ref, t, jnp.concatenate(proj[t], axis=0))
    store_proj = pltpu.make_async_copy(proj_ref, proj_out, s_o.at[1])
    store_proj.start()

    for t in range(3):
        same(pot_at(t, others, y, c), t_a.at[t], t_col.at[t, r], o_c).wait_send()
        same(pot_at(t, everyone, y, c), t_y.at[t], t_col.at[t, r], o_c).wait_send()
        same(pot_at(t, everyone, both, c), t_c.at[t], t_col.at[t, r], o_c).wait_send()

    grams.wait_send()

    store_pot.wait()
    store_proj.wait()


def on_device(orbitals, occupation):
    n_orb = lax.axis_size("orb")
    cols = n_orb // 4
    n = 2 * n_orb
    consts = tables()
    f32 = jnp.float32
    bf16 = jnp.bfloat16
    dma = pltpu.SemaphoreType.DMA
    vmem = pl.BlockSpec(memory_space=pltpu.VMEM)
    full = jax.ShapeDtypeStruct(orbitals.shape, f32)
    return pl.pallas_call(
        functools.partial(body, cols),
        out_shape=(full, full),
        in_specs=[vmem] * 2 + [pl.BlockSpec(memory_space=pl.ANY)] * 4,
        out_specs=(pl.BlockSpec(memory_space=pl.ANY),) * 2,
        scratch_shapes=[
            pltpu.VMEM(orbitals.shape, f32),
            pltpu.VMEM(orbitals.shape, f32),
            dma((2,)),
            *[pltpu.VMEM(a.shape, a.dtype) for a in consts],
            pltpu.VMEM((cols, 2, 2, 2, 3, TILE, PLANE), bf16),
            pltpu.VMEM((2, 3, TILE, PLANE), f32),
            pltpu.VMEM((2, 2, TILE, PLANE), f32),
            pltpu.VMEM((cols, 2, 2, 2, TILE, PLANE), f32),
            pltpu.VMEM((cols, 2, 2, 2 * EDGE, PLANE), f32),
            pltpu.VMEM((TILE, PLANE), bf16),
            pltpu.VMEM((TILE, PLANE), bf16),
            pltpu.VMEM((2, n, LANES), f32),
            pltpu.VMEM((2, n), f32),
            pltpu.VMEM((2 * n_orb, 2, n), f32),
            pltpu.VMEM((n, n), f32),
            dma((4,)),
            dma((2,)),
            dma((2,)),
            dma((3,)),
            dma((3,)),
            dma((3,)),
            dma((3, cols)),
            dma((3, cols)),
            dma((3, 2)),
            dma((2,)),
            dma((2,)),
            dma,
            dma,
            dma((3,)),
            dma((3,)),
            dma((3,)),
            dma((3, cols)),
            dma((3, cols)),
            dma((3, 2)),
        ],
        compiler_params=pltpu.CompilerParams(
            collective_id=0, has_side_effects=True, vmem_limit_bytes=60 * 1024 * 1024
        ),
        name="exchange",
    )(orbitals, occupation[None], *consts)


def solution(mesh):
    return jax.shard_map(
        on_device,
        mesh=mesh,
        in_specs=(P("orb", "grid"), P("orb")),
        out_specs=(P("orb", "grid"), P("orb", "grid")),
        check_vma=False,
    )
```

profile of v0, /device:TPU:0, one launch (start us, length us, event | category | flops | bytes accessed | tf_op | source)
XLA Modules:
  0.0 36.8 jit_solution(9333647089368861521)
XLA Ops:
  0.6 34.1 %exchange.1 = (f32[2,5760]{1,0:T(2,128)}, f32[2,5760]{1,0:T(2,128)}) custom-call(bf16[2,5760]{1,0:T(2,128)(2,1)} %own_ref.1, bf16[1,2]{1,0:T(2,128)(2,1)} %bitcast.1, bf16[192,192]{1,0:T(8,128)(2,1)} %constant.8.clone.tx_hbm, bf16[576,576]{1,0:T(8,128)(2,1)} %constant.9.clone.ty_hbm, bf16[384,384]{1,0:T(8,128)(2,1)} %constant.10.clone.tz_hbm, ...), custom_call_target="tpu_custom_call" | custom-call | tf_op jit(solution)/shard_map/exchange/pallas_call | solution.py:541
  34.7 0.0 copy-start
  34.7 1.4 %copy.10 = f32[2,5760]{1,0:T(2,128)} copy(f32[2,5760]{1,0:T(2,128)} %get-tuple-element.4) | data formatting | bytes 92160
  36.1 0.0 copy-done
  36.1 0.6 %copy.11 = f32[2,5760]{1,0:T(2,128)} copy(f32[2,5760]{1,0:T(2,128)S(1)} %copy-done) | data formatting | bytes 92160
Async XLA Ops:
  34.7 1.4 %copy-start = (f32[2,5760]{1,0:T(2,128)S(1)}, f32[2,5760]{1,0:T(2,128)}, u32[]{:S(2)}) copy-start(f32[2,5760]{1,0:T(2,128)} %get-tuple-element.5) | copy-start | bytes 138244
where the time goes:
time: 37 us; the launch traced here: 36.8 us
  Pallas kernels  34.1 us (92%)
  local copies, waits for them, and re-layouts  2.05 us (6%)
  between operations  0.65 us (2%)
    pallas_call x1, Pallas kernels, on_device(): pl.pallas_call(functools.partial(body, cols), out_shape=(full, full), in_...  34.1 us
    unnamed x4, local copies, waits for them, and re-layouts  2.05 us

commit v1 on v0

--- a/solution.py
+++ b/solution.py
@@ -20,7 +20,11 @@
 EDGE = HX - TILE
 ROWS = 3 * TILE
 LANES = 128
+PANEL = 8
 BATCH = 8
+GROUPS = 3
+GROUP = PLANE // GROUPS
+WIDE = 256
 MESH = pl.DeviceIdType.MESH
 
 
@@ -44,11 +48,18 @@
     return np.concatenate(parts, axis=0)
 
 
+def grouped(array):
+    rows = array.reshape((GROUPS, GROUP) + array.shape[1:])
+    wide = np.zeros((GROUPS, WIDE - GROUP) + array.shape[1:], array.dtype)
+    return np.concatenate([rows, wide], axis=1).reshape((GROUPS * WIDE,) + array.shape[1:])
+
+
 def tables():
-    table_x = padded_rows(padded_rows(hartley_table(NX)).T)
-    table_x = np.kron(np.eye(BATCH, dtype=np.float32), table_x)
-    table_y = np.kron(hartley_table(NY), np.eye(NZ, dtype=np.float32))
-    table_z = np.kron(np.eye(16, dtype=np.float32), hartley_table(NZ))
+    eye = np.eye(BATCH, dtype=np.float32)
+    table_x = padded_rows(hartley_table(NX))
+    table_y = grouped(np.kron(hartley_table(NY), np.eye(NZ, dtype=np.float32)))
+    table_z = np.zeros((WIDE, WIDE), np.float32)
+    table_z[:GROUP, :GROUP] = np.kron(np.eye(GROUP // NZ), hartley_table(NZ))
     total = (
         signed_square(NX)[:, None, None]
         + signed_square(NY)[None, :, None]
@@ -56,11 +67,16 @@
     )
     safe = np.where(total > 0, total, 1.0)
     kernel = np.where(total > 0, 1.0 / safe, 0.0) / NPTS
-    kernel = padded_rows(kernel.reshape(NX, PLANE).astype(np.float32))
+    kernel = grouped(kernel.reshape(NX, PLANE).astype(np.float32).T).T
+    kernel = kernel.reshape(NX, GROUPS, WIDE).transpose(1, 0, 2)
+    kernel = np.tile(kernel, (1, BATCH, 1))
+    bf16 = jnp.bfloat16
     return (
-        jnp.asarray(table_x, jnp.bfloat16),
-        jnp.asarray(table_y, jnp.bfloat16),
-        jnp.asarray(table_z, jnp.bfloat16),
+        jnp.asarray(np.kron(eye, table_x.T), bf16),
+        jnp.asarray(np.kron(eye, table_x), bf16),
+        jnp.asarray(table_y.T, bf16),
+        jnp.asarray(table_y, bf16),
+        jnp.asarray(table_z, bf16),
         jnp.asarray(kernel, jnp.float32),
     )
 
@@ -89,19 +105,23 @@
 
 def body(
     cols,
+    own_hbm,
+    occ_hbm,
+    xf_hbm,
+    xi_hbm,
+    yf_hbm,
+    yi_hbm,
+    tz_hbm,
+    k_hbm,
+    pot_ref,
+    proj_ref,
     own_ref,
     occ_ref,
-    tx_hbm,
-    ty_hbm,
-    tz_hbm,
-    k_hbm,
-    pot_out,
-    proj_out,
-    pot_ref,
-    proj_ref,
-    s_o,
-    tx_ref,
-    ty_ref,
+    s_own,
+    xf_ref,
+    xi_ref,
+    yf_ref,
+    yi_ref,
     tz_ref,
     k_ref,
     src,
@@ -116,21 +136,13 @@
     gall,
     gmat,
     s_tab,
-    s_x,
+    sent,
     r_x,
-    s_a,
-    s_y,
-    s_c,
     r_col,
     r_y,
     r_core,
-    s_p,
     r_p,
-    s_g,
     r_g,
-    t_a,
-    t_y,
-    t_c,
     t_col,
     t_yin,
     t_core,
@@ -148,15 +160,23 @@
     o_y = r * 4 + (1 - y) * 2 + c
     o_c = r * 4 + y * 2 + (1 - c)
 
+    inputs = [
+        pltpu.make_async_copy(a, b, s_own)
+        for a, b in ((own_hbm, own_ref), (occ_hbm, occ_ref))
+    ]
+    for load in inputs:
+        load.start()
     loads = [
-        pltpu.make_async_copy(a, b, s_tab.at[i])
-        for i, (a, b) in enumerate(
-            ((tx_hbm, tx_ref), (ty_hbm, ty_ref), (tz_hbm, tz_ref), (k_hbm, k_ref))
+        pltpu.make_async_copy(a, b, s_tab)
+        for a, b in (
+            (xf_hbm, xf_ref),
+            (yf_hbm, yf_ref),
+            (tz_hbm, tz_ref),
+            (k_hbm, k_ref),
+            (yi_hbm, yi_ref),
+            (xi_hbm, xi_ref),
         )
     ]
-    for load in loads:
-        load.start()
-
     barrier = pltpu.get_barrier_semaphore()
 
     def greet(orb, grid):
@@ -170,6 +190,10 @@
     greet(o_y, g)
     greet(o_c, g)
 
+    for load in loads:
+        load.start()
+    for load in inputs:
+        load.wait()
     own = own_ref[...].astype(f32)
     occ = occ_ref[...].astype(f32)
     own_edges = []
@@ -204,16 +228,16 @@
 
     def to_column(j, d):
         q = (r + d) % cols
-        return same(piece(j, r, y, c), s_a.at[j], r_col.at[j, r], q * 4 + y * 2 + c)
+        return same(piece(j, r, y, c), sent, r_col.at[j, r], q * 4 + y * 2 + c)
 
     def to_y(j, q):
-        return same(piece(j, q, y, c), s_y.at[j], r_y.at[j, q], o_y)
+        return same(piece(j, q, y, c), sent, r_y.at[j, q], o_y)
 
     def to_core(j, q, u):
-        return same(piece(j, q, u, c), s_c.at[j], r_core.at[j, u], o_c)
+        return same(piece(j, q, u, c), sent, r_core.at[j, u], o_c)
 
     def arrived(j, q, u, w, recv):
-        same(piece(j, q, u, w), s_a.at[j], recv, o_c).wait_recv()
+        same(piece(j, q, u, w), sent, recv, o_c).wait_recv()
 
     everyone = pl.ds(0, cols)
     others = pl.ds(0, cols - 1)
@@ -221,9 +245,9 @@
 
     def crossing(half):
         tile = src.at[r, y, c, :, 2 * half]
-        return copy(tile, tile, s_x.at[0], r_x.at[0], o, h)
-
-    crosses = (crossing(g), copy(edge_out, edge_in, s_x.at[1], r_x.at[1], o, h))
+        return copy(tile, tile, sent, r_x.at[0], o, h)
+
+    crosses = (crossing(g), copy(edge_out, edge_in, sent, r_x.at[1], o, h))
     for cross in crosses:
         cross.start()
 
@@ -277,65 +301,70 @@
     other_core(0, y)
     other_core(1, y)
 
-    tx = tx_ref[...]
-    ty = ty_ref[...]
+    xf = xf_ref[...]
+    xi = xi_ref[...]
+    yf = yf_ref[...]
+    yi = yi_ref[...]
     tz = tz_ref[...]
-    cut = tz.shape[0]
-    rest = PLANE - cut
     kern = k_ref[...]
 
     def mm(a, b):
         return jnp.dot(a, b, preferred_element_type=f32)
-
-    def along_z(a):
-        return jnp.concatenate([mm(a[:, :cut], tz), mm(a[:, cut:], tz[:rest, :rest])], axis=1)
 
     per = BATCH // 2
     block = (BATCH, ROWS, PLANE)
     flat_block = (BATCH * ROWS, PLANE)
     steps = cols // per
-
-    def one_batch(u, step, t, first):
+    slabs = BATCH * NX
+
+    def one_batch(u, step, ts, first):
         raw = src[pl.ds(step * per, per), u, :, g].reshape(BATCH * 3, TILE, PLANE)
         raw = raw.astype(f32).reshape(block)
         weight = raw[:, TILE + 2 * EDGE : TILE + 2 * EDGE + 1, :]
-        target = src[r, y, c, t].astype(f32).reshape(block[1:])
-        density = (raw * target[None]).reshape(flat_block).astype(bf16)
-        s = mm(tx, density).astype(bf16)
-        s = mm(s, ty).astype(bf16)
-        s = along_z(s).reshape(block) * kern[None]
-        s = along_z(s.reshape(flat_block).astype(bf16)).astype(bf16)
-        s = mm(s, ty).astype(bf16)
-        v = mm(tx, s).reshape(block)
-        total = jnp.sum(weight * v * raw, axis=0).reshape(3, TILE, PLANE)
+        parts = []
+        for t in ts:
+            target = src[r, y, c, t].astype(f32).reshape(block[1:])
+            density = (raw * target[None]).reshape(flat_block).astype(bf16)
+            parts.append(mm(xf, density).astype(bf16))
+        count = len(ts) * slabs
+        s = mm(jnp.concatenate(parts, axis=0), yf).astype(bf16)
+        s = [s[:, WIDE * k : WIDE * (k + 1)] for k in range(GROUPS)]
+        s = mm(jnp.concatenate(s, axis=0), tz)
+        s = s.reshape(GROUPS, len(ts), slabs, WIDE) * jnp.stack([kern] * len(ts), axis=1)
+        s = s.reshape(GROUPS * count, WIDE).astype(bf16)
+        s = mm(s, tz).astype(bf16)
+        s = [s[count * k : count * (k + 1)] for k in range(GROUPS)]
+        s = mm(jnp.concatenate(s, axis=1), yi).astype(bf16)
+        for k, t in enumerate(ts):
+            v = mm(xi, s[slabs * k : slabs * (k + 1)]).reshape(block)
+            total = jnp.sum(weight * v * raw, axis=0).reshape(3, TILE, PLANE)
+            if first:
+                part[t] = -total
+            else:
+                part[t] -= total
+
+    def batches(u, ts, first):
         if first:
-            part[t] = -total
-        else:
-            part[t] -= total
-
-    def batches(u, t, first):
-        if first:
-            one_batch(u, 0, t, True)
+            one_batch(u, 0, ts, True)
         if steps > int(first):
 
             @pl.loop(int(first), steps)
             def _(k):
-                one_batch(u, k, t, False)
-
-    batches(y, 0, True)
+                one_batch(u, k, ts, False)
+
+    batches(y, (0, 1), True)
     relay_y(0)
     relay_y(1)
-    batches(y, 1, True)
     relay_column(2)
     other_core(0, 1 - y)
     other_core(1, 1 - y)
-    batches(1 - y, 0, False)
+    batches(1 - y, (0,), False)
 
     def swap(t):
-        return copy(part.at[t, pl.ds(h, 2)], part_in.at[t], s_p.at[t], r_p.at[t], o, h)
+        return copy(part.at[t, pl.ds(h, 2)], part_in.at[t], sent, r_p.at[t], o, h)
 
     swap(0).start()
-    batches(1 - y, 1, False)
+    batches(1 - y, (1,), False)
     swap(1).start()
 
     relay_y(2)
@@ -345,16 +374,16 @@
 
     def pot_column(t, d):
         q = (r + d) % cols
-        return same(pot_at(t, r, y, c), t_a.at[t], t_col.at[t, r], q * 4 + y * 2 + c)
+        return same(pot_at(t, r, y, c), sent, t_col.at[t, r], q * 4 + y * 2 + c)
 
     def pot_y(t, q):
-        return same(pot_at(t, q, y, c), t_y.at[t], t_yin.at[t, q], o_y)
+        return same(pot_at(t, q, y, c), sent, t_yin.at[t, q], o_y)
 
     def pot_core(t, q, u):
-        return same(pot_at(t, q, u, c), t_c.at[t], t_core.at[t, u], o_c)
+        return same(pot_at(t, q, u, c), sent, t_core.at[t, u], o_c)
 
     def pot_arrived(t, q, u, w, recv):
-        same(pot_at(t, q, u, w), t_a.at[t], recv, o_c).wait_recv()
+        same(pot_at(t, q, u, w), sent, recv, o_c).wait_recv()
 
     def send_pots(t):
         @pl.loop(1, cols)
@@ -369,14 +398,15 @@
         def _(q):
             rows = src[q, :, :, :, 2 * g].reshape(8, TILE, PLANE).astype(f32)
             ends = src[q, :, :, :, 1].reshape(8, TILE, PLANE).astype(f32)
-            sums = jnp.sum(rows * value[0][None] + ends * value[2][None], axis=1)
-            fold = sums[:, :LANES]
+            sums = rows * value[0][None] + ends * value[2][None]
+            fold = sums[:, :, :LANES]
             for k in range(LANES, PLANE - LANES + 1, LANES):
-                fold += sums[:, k : k + LANES]
+                fold += sums[:, :, k : k + LANES]
             tail = PLANE % LANES
             if tail:
-                last = jnp.zeros((8, LANES - tail), f32)
-                fold += jnp.concatenate([sums[:, PLANE - tail :], last], axis=1)
+                last = jnp.zeros((8, TILE, LANES - tail), f32)
+                fold += jnp.concatenate([sums[:, :, PLANE - tail :], last], axis=2)
+            fold = jnp.sum(fold, axis=1)
             rowsum[t, pl.ds(pl.multiple_of(q * 8, 8), 8), :] = fold
 
         gown[t : t + 1, :] = jnp.sum(rowsum[t].T, axis=0, keepdims=True)
@@ -384,7 +414,7 @@
     def finish(t):
         swap(t).wait_recv()
         tile = part[t, 2 * g] + part_in[t, g]
-        pots[r, y, c, t] = tile
+        pots[r, y, c, t] = tile.astype(bf16)
         rest = part[t, 1] + part_in[t, h]
         edge = rest[:EDGE] * first_half + rest[EDGE : 2 * EDGE] * second_half
         line = lax.broadcasted_iota(jnp.int32, (TILE, PLANE), 0)
@@ -400,15 +430,27 @@
     gram_rows(1, value1)
     gall[g * n_orb + o] = gown[...]
 
-    def gram_to(d):
-        flat = (o * 2 + g + d) % (2 * n_orb)
-        return copy(gown, gall.at[g * n_orb + o], s_g, r_g, flat // 2, flat % 2)
-
-    @pl.loop(1, 2 * n_orb)
-    def _(d):
-        gram_to(d).start()
-
-    pedge[r, y, c] = jnp.concatenate([value0[1], value1[1]], axis=0)
+    def gram_to(dr, dy, dc, dg):
+        orb = (r + dr) % cols * 4 + (y + dy) % 2 * 2 + (c + dc) % 2
+        row = gall.at[g * n_orb + o]
+        return copy(gown, row, sent, r_g, orb, (g + dg) % 2)
+
+    corners = [(a, b, d) for a in (1, 0) for b in (1, 0) for d in (0, 1)]
+    if cols <= 4:
+        for dr in (cols - 1, *range(1, cols - 1), 0):
+            for corner in corners:
+                if (dr, *corner) != (0, 0, 0, 0):
+                    dy, dg, dc = corner
+                    gram_to(dr, dy, dc, dg).start()
+    else:
+        for dy, dg, dc in corners:
+            first = int((dy, dg, dc) == (0, 0, 0))
+
+            @pl.loop(first, cols)
+            def _(dr):
+                gram_to(dr, dy, dc, dg).start()
+
+    pedge[r, y, c] = jnp.concatenate([value0[1], value1[1]], axis=0).astype(bf16)
     send_pots(2)
 
     def write(ref, t, value):
@@ -418,8 +460,6 @@
 
     write(pot_ref, 0, jnp.concatenate(value0[:2], axis=0))
     write(pot_ref, 1, jnp.concatenate(value1[:2], axis=0))
-    store_pot = pltpu.make_async_copy(pot_ref, pot_out, s_o.at[0])
-    store_pot.start()
 
     def pot_relay_column(t):
         @pl.loop(1, cols)
@@ -441,18 +481,8 @@
     pot_relay_column(2)
     pot_relay_y(0)
 
-    for cross in crosses:
-        cross.wait_send()
-    for t in range(2):
-        swap(t).wait_send()
-
-    for j in range(3):
-        same(piece(j, others, y, c), s_a.at[j], r_col.at[j, r], o_c).wait_send()
-        same(piece(j, everyone, y, c), s_y.at[j], r_col.at[j, r], o_c).wait_send()
-        same(piece(j, everyone, both, c), s_c.at[j], r_col.at[j, r], o_c).wait_send()
-
     received = gall.at[pl.ds(0, 2 * n_orb - 1)]
-    grams = copy(received, received, s_g, r_g, o_c, g)
+    grams = copy(received, received, sent, r_g, o_c, g)
     grams.wait_recv()
 
     def assemble(k, carry):
@@ -475,57 +505,90 @@
         factor = jnp.where(below > k, column_of(left, k) * scale, 0.0)
         return left - factor * row_l, right - factor * row_of(right, k)
 
-    early = n * 3 // 4
-    if n <= 64:
-        pair = loop(early, eliminate, (sym, eye))
-        pot_relay_y(1)
-        pot_relay_y(2)
-        for k in range(early, n):
-            pair = eliminate(k, pair)
-        left, right = pair
+    def eliminate_panel(start, aug):
+        names = range(start, start + PANEL)
+        columns = [aug[:, k : k + 1] + jnp.zeros_like(aug) for k in names]
+        for i, k in enumerate(names):
+            scale = 1.0 / columns[i][k : k + 1]
+            factor = jnp.where(below > k, columns[i] * scale, 0.0)
+            aug = aug - factor * aug[k : k + 1]
+            for j in range(i + 1, PANEL):
+                columns[j] = columns[j] - factor * columns[j][k : k + 1]
+        return aug
+
+    if 2 * n <= LANES:
+        aug = jnp.concatenate([sym, eye], axis=1)
+        for k in range(0, n, PANEL):
+            aug = eliminate_panel(k, aug)
+            if k == n // 2:
+                pot_relay_y(1)
+                pot_relay_y(2)
+        left, right = aug[:, :n], aug[:, n:]
     else:
         pot_relay_y(1)
         pot_relay_y(2)
         left, right = loop(n, eliminate, (sym, eye))
-    diag = jnp.sum(left * eye, axis=1, keepdims=True)
-    inverse = right * (1.0 / jnp.sqrt(diag))
-    a0, a1 = row_of(inverse, 2 * o), row_of(inverse, 2 * o + 1)
+
+    def inverse_row(k):
+        diag = column_of(row_of(left, k), k)
+        return row_of(right, k) * (1.0 / jnp.sqrt(diag))
+
+    a0, a1 = inverse_row(2 * o), inverse_row(2 * o + 1)
 
     for u in range(2):
         for t in range(3):
             pot_arrived(t, everyone, u, 1 - c, t_core.at[t, u])
+
+    orbital = lax.broadcasted_iota(jnp.int32, (1, n), 1)
+    others0, others1 = [jnp.where(orbital // 2 == o, 0.0, a) for a in (a0, a1)]
 
     def add(k, sums):
         where = (k // 4, k % 4 // 2, k % 2)
         if not isinstance(k, int):
             where = (k // 4, lax.rem(k, 4) // 2, lax.rem(k, 2))
-        edge = pedge[where]
-        tiles = [pots[where + (t,)] for t in range(2)]
+        edge = pedge[where].astype(f32)
+        tiles = [pots[where + (t,)].astype(f32) for t in range(2)]
         ends = [edge[EDGE * t : EDGE * (t + 1)] for t in range(2)]
         new = []
-        for a, (tile, end) in zip((a0, a1), sums):
+        for a, (tile, end) in zip((others0, others1), sums):
             for t in range(2):
                 factor = column_of(a, 2 * k + t)
                 tile, end = tile + factor * tiles[t], end + factor * ends[t]
             new.append((tile, end))
         return tuple(new)
 
-    zero = (jnp.zeros((TILE, PLANE), f32), jnp.zeros((EDGE, PLANE), f32))
-    proj = loop(n_orb, add, (zero, zero))
+    def own_part(a):
+        f0, f1 = column_of(a, 2 * o), column_of(a, 2 * o + 1)
+        return tuple(f0 * v0 + f1 * v1 for v0, v1 in zip(value0[:2], value1[:2]))
+
+    proj = loop(n_orb, add, (own_part(a0), own_part(a1)))
     for t in range(2):
         write(proj_ref, t, jnp.concatenate(proj[t], axis=0))
-    store_proj = pltpu.make_async_copy(proj_ref, proj_out, s_o.at[1])
-    store_proj.start()
-
+
+    for cross in crosses:
+        cross.wait_send()
+    for t in range(2):
+        swap(t).wait_send()
+    for j in range(3):
+        same(piece(j, others, y, c), sent, r_col.at[j, r], o_c).wait_send()
+        same(piece(j, everyone, y, c), sent, r_col.at[j, r], o_c).wait_send()
+        same(piece(j, everyone, both, c), sent, r_col.at[j, r], o_c).wait_send()
     for t in range(3):
-        same(pot_at(t, others, y, c), t_a.at[t], t_col.at[t, r], o_c).wait_send()
-        same(pot_at(t, everyone, y, c), t_y.at[t], t_col.at[t, r], o_c).wait_send()
-        same(pot_at(t, everyone, both, c), t_c.at[t], t_col.at[t, r], o_c).wait_send()
-
+        same(pot_at(t, others, y, c), sent, t_col.at[t, r], o_c).wait_send()
+        same(pot_at(t, everyone, y, c), sent, t_col.at[t, r], o_c).wait_send()
+        same(pot_at(t, everyone, both, c), sent, t_col.at[t, r], o_c).wait_send()
     grams.wait_send()
 
-    store_pot.wait()
-    store_proj.wait()
+
+def store(pot_ref, proj_ref, pot_out, proj_out, sems):
+    copies = [
+        pltpu.make_async_copy(a, b, sems.at[i])
+        for i, (a, b) in enumerate(((pot_ref, pot_out), (proj_ref, proj_out)))
+    ]
+    for copy in copies:
+        copy.start()
+    for copy in copies:
+        copy.wait()
 
 
 def on_device(orbitals, occupation):
@@ -538,43 +601,36 @@
     dma = pltpu.SemaphoreType.DMA
     vmem = pl.BlockSpec(memory_space=pltpu.VMEM)
     full = jax.ShapeDtypeStruct(orbitals.shape, f32)
-    return pl.pallas_call(
+    held = pltpu.VMEM(orbitals.shape, f32)
+    pot, proj = pl.pallas_call(
         functools.partial(body, cols),
-        out_shape=(full, full),
-        in_specs=[vmem] * 2 + [pl.BlockSpec(memory_space=pl.ANY)] * 4,
-        out_specs=(pl.BlockSpec(memory_space=pl.ANY),) * 2,
+        out_shape=(held, held),
+        in_specs=[pl.BlockSpec(memory_space=pl.ANY)] * 8,
+        out_specs=(vmem, vmem),
         scratch_shapes=[
-            pltpu.VMEM(orbitals.shape, f32),
-            pltpu.VMEM(orbitals.shape, f32),
-            dma((2,)),
+            pltpu.VMEM(orbitals.shape, bf16),
+            pltpu.VMEM((1, 2), bf16),
+            dma,
             *[pltpu.VMEM(a.shape, a.dtype) for a in consts],
             pltpu.VMEM((cols, 2, 2, 2, 3, TILE, PLANE), bf16),
             pltpu.VMEM((2, 3, TILE, PLANE), f32),
             pltpu.VMEM((2, 2, TILE, PLANE), f32),
-            pltpu.VMEM((cols, 2, 2, 2, TILE, PLANE), f32),
-            pltpu.VMEM((cols, 2, 2, 2 * EDGE, PLANE), f32),
+            pltpu.VMEM((cols, 2, 2, 2, TILE, PLANE), bf16),
+            pltpu.VMEM((cols, 2, 2, 2 * EDGE, PLANE), bf16),
             pltpu.VMEM((TILE, PLANE), bf16),
             pltpu.VMEM((TILE, PLANE), bf16),
             pltpu.VMEM((2, n, LANES), f32),
             pltpu.VMEM((2, n), f32),
             pltpu.VMEM((2 * n_orb, 2, n), f32),
             pltpu.VMEM((n, n), f32),
-            dma((4,)),
+            dma,
+            dma,
             dma((2,)),
-            dma((2,)),
-            dma((3,)),
-            dma((3,)),
-            dma((3,)),
             dma((3, cols)),
             dma((3, cols)),
             dma((3, 2)),
             dma((2,)),
-            dma((2,)),
             dma,
-            dma,
-            dma((3,)),
-            dma((3,)),
-            dma((3,)),
             dma((3, cols)),
             dma((3, cols)),
             dma((3, 2)),
@@ -584,6 +640,15 @@
         ),
         name="exchange",
     )(orbitals, occupation[None], *consts)
+    anywhere = pl.BlockSpec(memory_space=pl.ANY)
+    return pl.pallas_call(
+        store,
+        out_shape=(full, full),
+        in_specs=[vmem, vmem],
+        out_specs=(anywhere, anywhere),
+        scratch_shapes=[dma((2,))],
+        name="store",
+    )(*[pltpu.with_memory_space_constraint(a, pltpu.VMEM) for a in (pot, proj)])
 
 
 def solution(mesh):

time: 37 us -> 31.7 us (0.86)
  Pallas kernels: 34.1 us -> 30.5 us
  local copies, waits for them, and re-layouts: 2.05 us -> 0 us
    pallas_call x1 -> x2, Pallas kernels: 34.1 us -> 30.5 us  [the longest x1 29.9 us: on_device(): pl.pallas_call(functools.partial(body, cols), out_shape=(held, held), in_...]
    unnamed x4 -> x0, local copies, waits for them, and re-layouts: 2.05 us -> none
where the time goes in v1:
time: 31.7 us; the launch traced here: 31.2 us
  Pallas kernels  30.5 us (96%)
  between operations  0.64 us (2%)
    pallas_call x1, Pallas kernels, on_device(): pl.pallas_call(functools.partial(body, cols), out_shape=(held, held), in_...  29.9 us
    pallas_call x1, Pallas kernels, on_device(): pl.pallas_call(store, out_shape=(full, full), in_specs=[vmem, vmem], out_...  0.65 us

profile of v1, /device:TPU:0, one launch (start us, length us, event | category | flops | bytes accessed | tf_op | source)
XLA Modules:
  0.0 31.2 jit_solution(4824144651080623708)
XLA Ops:
  0.6 29.9 %exchange.1 = (f32[2,5760]{1,0:T(2,128)S(1)}, f32[2,5760]{1,0:T(2,128)S(1)}) custom-call(bf16[2,5760]{1,0:T(2,128)(2,1)} %own_hbm.1, bf16[1,2]{1,0:T(2,128)(2,1)} %bitcast.1, bf16[160,192]{1,0:T(8,128)(2,1)} %constant.12.clone.xf_hbm, bf16[192,160]{1,0:T(8,128)(2,1)} %constant.13.clone.xi_hbm, bf16[576,768]{1,0:T(8,128)(2,1)} %constant.14.clone.yf_hbm, ...), custom_call_target="tpu_custom_call" | custom-call | tf_op jit(solution)/shard_map/exchange/pallas_call | solution.py:605
  30.5 0.7 %store.1 = (f32[2,5760]{1,0:T(2,128)}, f32[2,5760]{1,0:T(2,128)}) custom-call(f32[2,5760]{1,0:T(2,128)S(1)} %get-tuple-element.4.pot_ref, f32[2,5760]{1,0:T(2,128)S(1)} %get-tuple-element.5.proj_ref), custom_call_target="tpu_custom_call" | custom-call | tf_op jit(solution)/shard_map/store/pallas_call | solution.py:644
